TPU v7x, 32 devices: a whole 2x2x4 slice. The times are simulated.
32 devices in a mesh: gx: 2 (over y), gy: 4 (over x, core), gz: 4 (over z).
Axes of the slice: x: 2, y: 2, z: 4, core: 2. Of those that a mesh axis runs over, the one named last changes fastest.
Arguments:
- volume: float32 [16, 64, 512], P(('gx', 'gy'), None, 'gz'), may hold values from 0 to 1
- levels: int32 [4], replicated, may hold values from 0 to 255
Outputs:
- labelling: float32 [4, 16, 64, 512], P(None, 'gx', 'gy', 'gz')
- centers: float32 [4], replicated
All inputs are finite; a program needn't handle non-finite values.
Results may differ from a plain program's by a relative error of at most 0.0001.
Values sent between devices are 32-bit elements; how exact they have to be, the bound alone decides.
A program may use at most 64 MiB of HBM per device.

v0:
```python
import jax
import jax.numpy as jnp
from jax import lax
from jax.sharding import PartitionSpec as P

ITERS = 2
tau_step = 0.25
sigma_step = 0.25
smooth_weight = 0.5
prior_weight = 1.0


def with_halo(block, sides, width):
    for axis, dim in sides:
        count = lax.axis_size(axis)
        forward = [(i, i + 1) for i in range(count - 1)]
        backward = [(target, source) for source, target in forward]
        low = lax.ppermute(
            lax.slice_in_dim(block, block.shape[dim] - width, None, axis=dim), axis, forward
        )
        high = lax.ppermute(lax.slice_in_dim(block, 0, width, axis=dim), axis, backward)
        block = jnp.concatenate([low, block, high], axis=dim)
    return block


def project_simplex(values):
    how_many = values.shape[0]
    threshold = None
    for subset in range(1, 1 << how_many):
        members = [label_index for label_index in range(how_many) if subset >> label_index & 1]
        summed = values[members[0]]
        for label_index in members[1:]:
            summed = summed + values[label_index]
        candidate = (summed - 1.0) / float(len(members))
        threshold = candidate if threshold is None else jnp.maximum(threshold, candidate)
    return jnp.maximum(values - threshold[None], 0.0)


def bounds(start, total, extent):
    position = start - 1 + jnp.arange(extent + 1, dtype=jnp.int32)
    return (position >= 0, position < total - 1)


def local(volume, levels):
    thickness = volume.shape[0]
    x_start = (lax.axis_index("gx") * lax.axis_size("gy") + lax.axis_index("gy")) * thickness
    x_total = thickness * lax.axis_size("gx") * lax.axis_size("gy")
    y_start = 0
    y_total = volume.shape[1]
    z_start = lax.axis_index("gz") * volume.shape[2]
    z_total = volume.shape[2] * lax.axis_size("gz")
    extent = volume.shape
    how_many = levels.shape[0]
    inside_x, ahead_x = bounds(x_start, x_total, extent[0])
    inside_y, ahead_y = bounds(y_start, y_total, extent[1])
    inside_z, ahead_z = bounds(z_start, z_total, extent[2])
    inside = (inside_x[:, None, None] & inside_y[None, :, None] & inside_z[None, None, :]).astype(
        jnp.float32
    )
    base_levels = levels.astype(jnp.float32) / 255.0
    centers = base_levels
    starting = (volume[None] - base_levels[:, None, None, None]) ** 2
    labelling = project_simplex(1.0 / how_many - tau_step * starting)
    smoothed = labelling
    dual_field = jnp.zeros((how_many, 3, extent[0] + 1, extent[1] + 1, extent[2] + 1), jnp.float32)
    for iteration in range(ITERS):
        padded = with_halo(smoothed, ((("gx", "gy"), 1), ("gz", 3)), 1)
        padded = jnp.pad(padded, ((0, 0), (0, 0), (1, 1), (0, 0)))
        corner = padded[:, :-1, :-1, :-1]
        grad_x = jnp.where(ahead_x[:, None, None], padded[:, 1:, :-1, :-1] - corner, 0.0)
        grad_y = jnp.where(ahead_y[None, :, None], padded[:, :-1, 1:, :-1] - corner, 0.0)
        grad_z = jnp.where(ahead_z[None, None, :], padded[:, :-1, :-1, 1:] - corner, 0.0)
        stepped = dual_field + sigma_step * jnp.stack([grad_x, grad_y, grad_z], axis=1)
        length = jnp.sqrt(
            stepped[:, 0] * stepped[:, 0]
            + stepped[:, 1] * stepped[:, 1]
            + stepped[:, 2] * stepped[:, 2]
        )
        shrink = inside / jnp.maximum(1.0, length / smooth_weight)
        dual_field = stepped * shrink[:, None]
        divergence = (
            dual_field[:, 0, 1:, 1:, 1:]
            - dual_field[:, 0, :-1, 1:, 1:]
            + (dual_field[:, 1, 1:, 1:, 1:] - dual_field[:, 1, 1:, :-1, 1:])
            + (dual_field[:, 2, 1:, 1:, 1:] - dual_field[:, 2, 1:, 1:, :-1])
        )
        fidelity = (volume[None] - centers[:, None, None, None]) ** 2
        updated = project_simplex(labelling + tau_step * (divergence - fidelity))
        smoothed = 2.0 * updated - labelling
        labelling = updated
        sizes_local = jnp.sum(labelling, axis=(1, 2, 3))
        weighted = jnp.sum(labelling * volume[None], axis=(1, 2, 3))
        sizes_all, weighted_all = lax.psum((sizes_local, weighted), ("gx", "gy", "gz"))
        centers = (weighted_all + prior_weight * base_levels) / (sizes_all + prior_weight)
    labelling = lax.all_to_all(labelling, "gy", split_axis=2, concat_axis=1, tiled=True)
    return (labelling, centers)


def solution(mesh):
    return jax.shard_map(
        local,
        mesh=mesh,
        in_specs=(P(("gx", "gy"), None, "gz"), P()),
        out_specs=(P(None, "gx", "gy", "gz"), P()),
        check_vma=False,
    )
```

profile of v0, /device:TPU:0, one launch (start us, length us, event | category | flops | bytes accessed | tf_op | source)
XLA Modules:
  0.0 159.2 jit_solution(3588290688517704985)
XLA Ops:
  1.3 0.9 multiply_subtract_fusion.1
  3.0 1.0 subtract_maximum_fusion.2
  4.0 2.4 %collective-permute-start = (f32[4,1,64,128]{3,2,1,0:T(8,128)S(1)}, f32[4,1,64,128]{3,2,1,0:T(8,128)S(1)}, u32[]{:S(2)}, u32[]{:S(2)}) collective-permute-start(f32[4,1,64,128]{3,2,1,0:T(8,128)S(1)} %get-tuple-element.24), channel_id=1, source_target_pairs={{0,4},{4,8},{8,12},{12,16},{16,20},{20,24},{24,28},{1,5},{5,9},{9,... | collective-permute-start | bytes 393224 | tf_op jit(solution)/shard_map/ppermute | solution.py:18
  6.4 1.3 collective-permute-start.1
  8.0 3.7 %collective-permute-done.1 = f32[4,1,64,128]{3,2,1,0:T(8,128)S(1)} collective-permute-done((f32[4,1,64,128]{3,2,1,0:T(8,128)S(1)}, f32[4,1,64,128]{3,2,1,0:T(8,128)S(1)}, u32[]{:S(2)}, u32[]{:S(2)}) %collective-permute-start.1) | collective-permute-done | bytes 131104 | tf_op jit(solution)/shard_map/ppermute | solution.py:21
  12.0 3.5 %collective-permute-start.2 = (f32[4,4,64,1]{3,2,1,0:T(8,128)S(1)}, f32[4,4,64,1]{3,2,1,0:T(8,128)S(1)}, u32[]{:S(2)}, u32[]{:S(2)}) collective-permute-start(f32[4,4,64,1]{3,2,1,0:T(8,128)S(1)} %get-tuple-element.19), channel_id=1, source_target_pairs={{0,1},{1,2},{2,3},{4,5},{5,6},{6,7},{8,9},{9,10},{10,11},{12,13},{... | collective-permute-start | bytes 12296 | tf_op jit(solution)/shard_map/ppermute | solution.py:18
  15.5 1.3 collective-permute-start.3
  16.8 8.4 %collective-permute-done.2 = f32[4,4,64,1]{3,2,1,0:T(8,128)S(1)} collective-permute-done((f32[4,4,64,1]{3,2,1,0:T(8,128)S(1)}, f32[4,4,64,1]{3,2,1,0:T(8,128)S(1)}, u32[]{:S(2)}, u32[]{:S(2)}) %collective-permute-start.2) | collective-permute-done | bytes 4128 | tf_op jit(solution)/shard_map/ppermute | solution.py:18
  25.2 4.7 %collective-permute-done.3 = f32[4,4,64,1]{3,2,1,0:T(8,128)S(1)} collective-permute-done((f32[4,4,64,1]{3,2,1,0:T(8,128)S(1)}, f32[4,4,64,1]{3,2,1,0:T(8,128)S(1)}, u32[]{:S(2)}, u32[]{:S(2)}) %collective-permute-start.3) | collective-permute-done | bytes 4128 | tf_op jit(solution)/shard_map/ppermute | solution.py:21
  33.1 0.9 copy-done
  34.1 1.1 multiply_reduce_fusion.1
  36.6 4.7 %collective-permute-start.4 = (f32[4,1,64,128]{3,2,1,0:T(8,128)}, f32[4,1,64,128]{3,2,1,0:T(8,128)}, u32[]{:S(2)}, u32[]{:S(2)}) collective-permute-start(f32[4,1,64,128]{3,2,1,0:T(8,128)} %get-tuple-element.22), channel_id=1, source_target_pairs={{0,4},{4,8},{8,12},{12,16},{16,20},{20,24},{24,28},{1,5},{5,9},{9,... | collective-permute-start | bytes 393224 | tf_op jit(solution)/shard_map/ppermute | solution.py:18
  41.3 1.3 collective-permute-start.5
  42.6 44.4 %all-reduce.3 = (f32[4]{0:T(128)}, f32[4]{0:T(128)}) all-reduce(f32[4]{0:T(128)} %get-tuple-element.3, f32[4]{0:T(128)} %get-tuple-element.2), channel_id=1, replica_groups=mesh['gx'=2,'gy'=4,'gz'=4] {'gx','gy','gz'}, use_global_device_ids=true, to_apply=%region_3.4 | all-reduce | flops 8 | bytes 64 | tf_op jit(solution)/shard_map/psum | solution.py:93
  87.0 1.1 pad_maximum_fusion.2
  88.4 2.3 %collective-permute-start.6 = (f32[4,4,64,1]{3,2,1,0:T(8,128)S(1)}, f32[4,4,64,1]{3,2,1,0:T(8,128)S(1)}, u32[]{:S(2)}, u32[]{:S(2)}) collective-permute-start(f32[4,4,64,1]{3,2,1,0:T(8,128)S(1)} %get-tuple-element.17), channel_id=1, source_target_pairs={{0,1},{1,2},{2,3},{4,5},{5,6},{6,7},{8,9},{9,10},{10,11},{12,13},{... | collective-permute-start | bytes 12296 | tf_op jit(solution)/shard_map/ppermute | solution.py:18
  90.7 1.3 collective-permute-start.7
  92.1 9.2 %collective-permute-done.6 = f32[4,4,64,1]{3,2,1,0:T(8,128)S(1)} collective-permute-done((f32[4,4,64,1]{3,2,1,0:T(8,128)S(1)}, f32[4,4,64,1]{3,2,1,0:T(8,128)S(1)}, u32[]{:S(2)}, u32[]{:S(2)}) %collective-permute-start.6) | collective-permute-done | bytes 4128 | tf_op jit(solution)/shard_map/ppermute | solution.py:18
  101.3 4.1 %collective-permute-done.7 = f32[4,4,64,1]{3,2,1,0:T(8,128)S(1)} collective-permute-done((f32[4,4,64,1]{3,2,1,0:T(8,128)S(1)}, f32[4,4,64,1]{3,2,1,0:T(8,128)S(1)}, u32[]{:S(2)}, u32[]{:S(2)}) %collective-permute-start.7) | collective-permute-done | bytes 4128 | tf_op jit(solution)/shard_map/ppermute | solution.py:21
  105.5 1.5 select_maximum_fusion
  109.4 1.2 copy-done.1
  111.6 0.9 copy.8
  112.5 3.9 %all-to-all-start = ((f32[4,2,64,128]{3,1,0,2:T(2,128)}), f32[4,2,64,128]{3,1,0,2:T(2,128)S(1)}, u32[]{:S(2)}, u32[]{:S(2)}) async-start(f32[4,2,64,128]{3,1,0,2:T(2,128)} %copy.8), calls=%async_computation | async-start | bytes 524288 | tf_op jit(solution)/shard_map/all_to_all | solution.py:95
  116.4 41.5 %all-reduce.2 = (f32[4]{0:T(128)S(1)}, f32[4]{0:T(128)S(1)}) all-reduce(f32[4]{0:T(128)S(1)} %get-tuple-element.5, f32[4]{0:T(128)S(1)} %get-tuple-element.4), channel_id=1, replica_groups=mesh['gx'=2,'gy'=4,'gz'=4] {'gx','gy','gz'}, use_global_device_ids=true, to_apply=%region_7.8 | all-reduce | flops 8 | bytes 64 | tf_op jit(solution)/shard_map/psum | solution.py:93
  (71 shorter events, 11.4 us)
Async XLA Ops:
  4.0 4.0 %collective-permute-start = (f32[4,1,64,128]{3,2,1,0:T(8,128)S(1)}, f32[4,1,64,128]{3,2,1,0:T(8,128)S(1)}, u32[]{:S(2)}, u32[]{:S(2)}) collective-permute-start(f32[4,1,64,128]{3,2,1,0:T(8,128)S(1)} %get-tuple-element.24), channel_id=1, source_target_pairs={{0,4},{4,8},{8,12},{12,16},{16,20},{20,24},{24,28},{1,5},{5,9},{9,... | collective-permute-start | bytes 393224 | tf_op jit(solution)/shard_map/ppermute | solution.py:18
  6.4 5.3 %collective-permute-start.1 = (f32[4,1,64,128]{3,2,1,0:T(8,128)S(1)}, f32[4,1,64,128]{3,2,1,0:T(8,128)S(1)}, u32[]{:S(2)}, u32[]{:S(2)}) collective-permute-start(f32[4,1,64,128]{3,2,1,0:T(8,128)S(1)} %get-tuple-element.25), channel_id=1, source_target_pairs={{4,0},{8,4},{12,8},{16,12},{20,16},{24,20},{28,24},{5,1},{9,5},{13... | collective-permute-start | bytes 393224 | tf_op jit(solution)/shard_map/ppermute | solution.py:21
  7.9 23.2 %copy-start.6 = (f32[3,65,129]{2,1,0:T(8,128)}, f32[3,65,129]{2,1,0:T(8,128)S(1)}, u32[]{:S(2)}) copy-start(f32[3,65,129]{2,1,0:T(8,128)S(1)} %and_convert_fusion) | copy-start | bytes 301864
  12.0 13.2 %collective-permute-start.2 = (f32[4,4,64,1]{3,2,1,0:T(8,128)S(1)}, f32[4,4,64,1]{3,2,1,0:T(8,128)S(1)}, u32[]{:S(2)}, u32[]{:S(2)}) collective-permute-start(f32[4,4,64,1]{3,2,1,0:T(8,128)S(1)} %get-tuple-element.19), channel_id=1, source_target_pairs={{0,1},{1,2},{2,3},{4,5},{5,6},{6,7},{8,9},{9,10},{10,11},{12,13},{... | collective-permute-start | bytes 12296 | tf_op jit(solution)/shard_map/ppermute | solution.py:18
  15.5 14.4 %collective-permute-start.3 = (f32[4,4,64,1]{3,2,1,0:T(8,128)S(1)}, f32[4,4,64,1]{3,2,1,0:T(8,128)S(1)}, u32[]{:S(2)}, u32[]{:S(2)}) collective-permute-start(f32[4,4,64,1]{3,2,1,0:T(8,128)S(1)} %get-tuple-element.20), channel_id=1, source_target_pairs={{1,0},{2,1},{3,2},{5,4},{6,5},{7,6},{9,8},{10,9},{11,10},{13,12},{... | collective-permute-start | bytes 12296 | tf_op jit(solution)/shard_map/ppermute | solution.py:21
  16.8 14.1 %copy-start.14 = (pred[65]{0:T(512)(128)(4,1)}, pred[65]{0:T(512)(128)(4,1)S(1)}, u32[]{:S(2)}) copy-start(pred[65]{0:T(512)(128)(4,1)S(1)} %fusion.62) | copy-start | bytes 199
  31.7 0.9 copy-start.9
  32.5 1.5 copy-start
  34.1 2.6 %copy-start.11 = (f32[2,64,128]{2,1,0:T(8,128)}, f32[2,64,128]{2,1,0:T(8,128)S(1)}, u32[]{:S(2)}) copy-start(f32[2,64,128]{2,1,0:T(8,128)S(1)} %maximum_bitcast_fusion.1) | copy-start | bytes 196612
  34.1 58.0 %copy-start.13 = (s32[4]{0:T(128)S(1)}, s32[4]{0:T(128)}, u32[]{:S(2)}) copy-start(s32[4]{0:T(128)} %param.3) | copy-start | bytes 52
  36.6 50.4 %collective-permute-start.4 = (f32[4,1,64,128]{3,2,1,0:T(8,128)}, f32[4,1,64,128]{3,2,1,0:T(8,128)}, u32[]{:S(2)}, u32[]{:S(2)}) collective-permute-start(f32[4,1,64,128]{3,2,1,0:T(8,128)} %get-tuple-element.22), channel_id=1, source_target_pairs={{0,4},{4,8},{8,12},{12,16},{16,20},{20,24},{24,28},{1,5},{5,9},{9,... | collective-permute-start | bytes 393224 | tf_op jit(solution)/shard_map/ppermute | solution.py:18
  41.3 45.7 %collective-permute-start.5 = (f32[4,1,64,128]{3,2,1,0:T(8,128)}, f32[4,1,64,128]{3,2,1,0:T(8,128)}, u32[]{:S(2)}, u32[]{:S(2)}) collective-permute-start(f32[4,1,64,128]{3,2,1,0:T(8,128)} %get-tuple-element.23), channel_id=1, source_target_pairs={{4,0},{8,4},{12,8},{16,12},{20,16},{24,20},{28,24},{5,1},{9,5},{13... | collective-permute-start | bytes 393224 | tf_op jit(solution)/shard_map/ppermute | solution.py:21
  87.0 5.0 %copy-start.16 = (f32[4]{0:T(128)S(1)}, f32[4]{0:T(128)}, u32[]{:S(2)}) copy-start(f32[4]{0:T(128)} %get-tuple-element.8) | copy-start | bytes 52
  87.0 5.0 %copy-start.17 = (f32[4]{0:T(128)S(1)}, f32[4]{0:T(128)}, u32[]{:S(2)}) copy-start(f32[4]{0:T(128)} %get-tuple-element.9) | copy-start | bytes 52
  87.0 18.4 %copy-start.3 = (f32[4,2,64,128]{3,2,1,0:T(8,128)S(1)}, f32[4,2,64,128]{3,2,1,0:T(8,128)}, u32[]{:S(2)}) copy-start(f32[4,2,64,128]{3,2,1,0:T(8,128)} %copy-done.2) | copy-start | bytes 786436
  88.2 18.8 %copy-start.15 = (pred[65]{0:T(512)(128)(4,1)S(1)}, pred[65]{0:T(512)(128)(4,1)}, u32[]{:S(2)}) copy-start(pred[65]{0:T(512)(128)(4,1)} %copy-done.14) | copy-start | bytes 199
  88.4 12.9 %collective-permute-start.6 = (f32[4,4,64,1]{3,2,1,0:T(8,128)S(1)}, f32[4,4,64,1]{3,2,1,0:T(8,128)S(1)}, u32[]{:S(2)}, u32[]{:S(2)}) collective-permute-start(f32[4,4,64,1]{3,2,1,0:T(8,128)S(1)} %get-tuple-element.17), channel_id=1, source_target_pairs={{0,1},{1,2},{2,3},{4,5},{5,6},{6,7},{8,9},{9,10},{10,11},{12,13},{... | collective-permute-start | bytes 12296 | tf_op jit(solution)/shard_map/ppermute | solution.py:18
  90.7 14.7 %collective-permute-start.7 = (f32[4,4,64,1]{3,2,1,0:T(8,128)S(1)}, f32[4,4,64,1]{3,2,1,0:T(8,128)S(1)}, u32[]{:S(2)}, u32[]{:S(2)}) collective-permute-start(f32[4,4,64,1]{3,2,1,0:T(8,128)S(1)} %get-tuple-element.18), channel_id=1, source_target_pairs={{1,0},{2,1},{3,2},{5,4},{6,5},{7,6},{9,8},{10,9},{11,10},{13,12},{... | collective-permute-start | bytes 12296 | tf_op jit(solution)/shard_map/ppermute | solution.py:21
  107.4 0.9 copy-start.7
  108.8 1.8 %copy-start.1 = (f32[4,3,3,65,129]{4,3,2,0,1:T(8,128)S(1)}, f32[4,3,3,65,129]{4,3,2,0,1:T(8,128)}, u32[]{:S(2)}) copy-start(f32[4,3,3,65,129]{4,3,2,0,1:T(8,128)} %copy-done) | copy-start | bytes 3622324
  108.8 1.7 %copy-start.5 = (f32[2,64,128]{2,1,0:T(8,128)S(1)}, f32[2,64,128]{2,1,0:T(8,128)}, u32[]{:S(2)}) copy-start(f32[2,64,128]{2,1,0:T(8,128)} %param.2) | copy-start | bytes 196612
  108.8 1.7 %copy-start.10 = (f32[2,64,128]{2,1,0:T(8,128)S(1)}, f32[2,64,128]{2,1,0:T(8,128)}, u32[]{:S(2)}) copy-start(f32[2,64,128]{2,1,0:T(8,128)} %copy-done.8) | copy-start | bytes 196612
  108.8 1.7 %copy-start.12 = (f32[2,64,128]{2,1,0:T(8,128)S(1)}, f32[2,64,128]{2,1,0:T(8,128)}, u32[]{:S(2)}) copy-start(f32[2,64,128]{2,1,0:T(8,128)} %copy-done.11) | copy-start | bytes 196612
  112.5 45.9 %all-to-all-start = ((f32[4,2,64,128]{3,1,0,2:T(2,128)}), f32[4,2,64,128]{3,1,0,2:T(2,128)S(1)}, u32[]{:S(2)}, u32[]{:S(2)}) async-start(f32[4,2,64,128]{3,1,0,2:T(2,128)} %copy.8), calls=%async_computation | async-start | bytes 524288 | tf_op jit(solution)/shard_map/all_to_all | solution.py:95
  (3 other events, 2.2 us)
where the time goes:
time: 160 us; the launch traced here: 159 us
  blocking collectives  85.9 us (54%)
  waiting for transfers between devices  30.2 us (19%)
  starting transfers between devices  22 us (14%)
  other arithmetic  12.8 us (8%)
  local copies, waits for them, and re-layouts  7.36 us (5%)
    psum x2, blocking collectives, local(): lax.psum((sizes_local, weighted), ('gx', 'gy', 'gz'))  85.9 us
    ppermute x4, waiting for transfers between devices, with_halo(): lax.ppermute(lax.slice_in_dim(block, block.shape[dim] - width, None, axis...  17.6 us
    ppermute x4, starting transfers between devices, with_halo(): lax.ppermute(lax.slice_in_dim(block, block.shape[dim] - width, None, axis...  12.9 us
    ppermute x4, waiting for transfers between devices, with_halo(): lax.ppermute(lax.slice_in_dim(block, 0, width, axis=dim), axis, backward)  12.6 us
    ppermute x4, starting transfers between devices, with_halo(): lax.ppermute(lax.slice_in_dim(block, 0, width, axis=dim), axis, backward)  5.16 us
    unnamed x36, local copies, waits for them, and re-layouts  4.51 us
    all_to_all x1, starting transfers between devices, local(): lax.all_to_all(labelling, 'gy', split_axis=2, concat_axis=1, tiled=True)  3.9 us
  transfers between devices with their start and end apart: 9, of which 5 were waited for; matrix products, arithmetic and copies ran while one was open for 0% of the time, Pallas kernels for 0%

commit v1 on v0

--- a/solution.py
+++ b/solution.py
@@ -90,7 +90,7 @@
         labelling = updated
         sizes_local = jnp.sum(labelling, axis=(1, 2, 3))
         weighted = jnp.sum(labelling * volume[None], axis=(1, 2, 3))
-        sizes_all, weighted_all = lax.psum((sizes_local, weighted), ("gx", "gy", "gz"))
+        sizes_all, weighted_all = lax.psum(lax.psum((sizes_local, weighted), ("gy", "gz")), "gx")
         centers = (weighted_all + prior_weight * base_levels) / (sizes_all + prior_weight)
     labelling = lax.all_to_all(labelling, "gy", split_axis=2, concat_axis=1, tiled=True)
     return (labelling, centers)

time: 160 us -> 149 us (0.931)
  blocking collectives: 85.9 us -> 78.4 us
  waiting for transfers between devices: 30.2 us -> 26.6 us
    psum x2 -> x4, blocking collectives: 85.9 us -> 78.4 us  [the longest x2 67.8 us: local(): lax.psum((sizes_local, weighted), ('gy', 'gz'))]
    ppermute x4, waiting for transfers between devices: 17.6 us -> 13.9 us  [with_halo(): lax.ppermute(lax.slice_in_dim(block, block.shape[dim] - width, None, axis...]
  transfers between devices with their start and end apart: 9 -> 9, of which waited for: 5 -> 5; matrix products, arithmetic and copies ran while one was open for 0% -> 1% of each run, Pallas kernels for 0% -> 0%
where the time goes in v1:
time: 149 us; the launch traced here: 148 us
  blocking collectives  78.4 us (53%)
  waiting for transfers between devices  26.6 us (18%)
  starting transfers between devices  21.8 us (15%)
  other arithmetic  12.8 us (9%)
  local copies, waits for them, and re-layouts  7.37 us (5%)
    psum x2, blocking collectives, local(): lax.psum((sizes_local, weighted), ('gy', 'gz'))  67.8 us
    ppermute x4, waiting for transfers between devices, with_halo(): lax.ppermute(lax.slice_in_dim(block, block.shape[dim] - width, None, axis...  13.9 us
    ppermute x4, starting transfers between devices, with_halo(): lax.ppermute(lax.slice_in_dim(block, block.shape[dim] - width, None, axis...  13.2 us
    ppermute x4, waiting for transfers between devices, with_halo(): lax.ppermute(lax.slice_in_dim(block, 0, width, axis=dim), axis, backward)  12.7 us
    psum x2, blocking collectives, local(): lax.psum(lax.psum((sizes_local, weighted), ('gy', 'gz')), 'gx')  10.5 us
    ppermute x4, starting transfers between devices, with_halo(): lax.ppermute(lax.slice_in_dim(block, 0, width, axis=dim), axis, backward)  5.16 us
    unnamed x36, local copies, waits for them, and re-layouts  4.52 us
    all_to_all x1, starting transfers between devices, local(): lax.all_to_all(labelling, 'gy', split_axis=2, concat_axis=1, tiled=True)  3.41 us
  transfers between devices with their start and end apart: 9, of which 5 were waited for; matrix products, arithmetic and copies ran while one was open for 1% of the time, Pallas kernels for 0%

profile of v1, /device:TPU:0, one launch (start us, length us, event | category | flops | bytes accessed | tf_op | source)
XLA Modules:
  0.0 147.9 jit_solution(13220926109001378380)
XLA Ops:
  1.3 0.9 multiply_subtract_fusion.1
  3.0 1.0 subtract_maximum_fusion.2
  4.0 2.4 %collective-permute-start = (f32[4,1,64,128]{3,2,1,0:T(8,128)S(1)}, f32[4,1,64,128]{3,2,1,0:T(8,128)S(1)}, u32[]{:S(2)}, u32[]{:S(2)}) collective-permute-start(f32[4,1,64,128]{3,2,1,0:T(8,128)S(1)} %get-tuple-element.28), channel_id=1, source_target_pairs={{0,4},{4,8},{8,12},{12,16},{16,20},{20,24},{24,28},{1,5},{5,9},{9,... | collective-permute-start | bytes 393224 | tf_op jit(solution)/shard_map/ppermute | solution.py:18
  6.4 1.3 collective-permute-start.1
  8.0 3.7 %collective-permute-done.1 = f32[4,1,64,128]{3,2,1,0:T(8,128)S(1)} collective-permute-done((f32[4,1,64,128]{3,2,1,0:T(8,128)S(1)}, f32[4,1,64,128]{3,2,1,0:T(8,128)S(1)}, u32[]{:S(2)}, u32[]{:S(2)}) %collective-permute-start.1) | collective-permute-done | bytes 131104 | tf_op jit(solution)/shard_map/ppermute | solution.py:21
  12.0 3.5 %collective-permute-start.2 = (f32[4,4,64,1]{3,2,1,0:T(8,128)S(1)}, f32[4,4,64,1]{3,2,1,0:T(8,128)S(1)}, u32[]{:S(2)}, u32[]{:S(2)}) collective-permute-start(f32[4,4,64,1]{3,2,1,0:T(8,128)S(1)} %get-tuple-element.23), channel_id=1, source_target_pairs={{0,1},{1,2},{2,3},{4,5},{5,6},{6,7},{8,9},{9,10},{10,11},{12,13},{... | collective-permute-start | bytes 12296 | tf_op jit(solution)/shard_map/ppermute | solution.py:18
  15.5 1.3 collective-permute-start.3
  16.8 8.4 %collective-permute-done.2 = f32[4,4,64,1]{3,2,1,0:T(8,128)S(1)} collective-permute-done((f32[4,4,64,1]{3,2,1,0:T(8,128)S(1)}, f32[4,4,64,1]{3,2,1,0:T(8,128)S(1)}, u32[]{:S(2)}, u32[]{:S(2)}) %collective-permute-start.2) | collective-permute-done | bytes 4128 | tf_op jit(solution)/shard_map/ppermute | solution.py:18
  25.2 4.7 %collective-permute-done.3 = f32[4,4,64,1]{3,2,1,0:T(8,128)S(1)} collective-permute-done((f32[4,4,64,1]{3,2,1,0:T(8,128)S(1)}, f32[4,4,64,1]{3,2,1,0:T(8,128)S(1)}, u32[]{:S(2)}, u32[]{:S(2)}) %collective-permute-start.3) | collective-permute-done | bytes 4128 | tf_op jit(solution)/shard_map/ppermute | solution.py:21
  34.1 1.2 multiply_reduce_fusion.1
  36.7 4.7 %collective-permute-start.4 = (f32[4,1,64,128]{3,2,1,0:T(8,128)}, f32[4,1,64,128]{3,2,1,0:T(8,128)}, u32[]{:S(2)}, u32[]{:S(2)}) collective-permute-start(f32[4,1,64,128]{3,2,1,0:T(8,128)} %get-tuple-element.26), channel_id=1, source_target_pairs={{0,4},{4,8},{8,12},{12,16},{16,20},{20,24},{24,28},{1,5},{5,9},{9,... | collective-permute-start | bytes 393224 | tf_op jit(solution)/shard_map/ppermute | solution.py:18
  41.3 1.3 collective-permute-start.5
  42.6 36.5 %all-reduce.3 = (f32[4]{0:T(128)}, f32[4]{0:T(128)}) all-reduce(f32[4]{0:T(128)} %get-tuple-element.3, f32[4]{0:T(128)} %get-tuple-element.2), channel_id=1, replica_groups=mesh['gx'=2,'gy'=4,'gz'=4] {'gy','gz'}, use_global_device_ids=true, to_apply=%region_4.5 | all-reduce | flops 8 | bytes 64 | tf_op jit(solution)/shard_map/psum | solution.py:93
  79.1 5.6 %all-reduce.5 = (f32[4]{0:T(128)}, f32[4]{0:T(128)}) all-reduce(f32[4]{0:T(128)} %get-tuple-element.8, f32[4]{0:T(128)} %get-tuple-element.9), channel_id=1, replica_groups=mesh['gx'=2,'gy'=4,'gz'=4] {'gx'}, use_global_device_ids=true, to_apply=%region_5.6 | all-reduce | flops 8 | bytes 64 | tf_op jit(solution)/shard_map/psum | solution.py:93
  84.7 1.1 pad_maximum_fusion.2
  86.1 2.6 %collective-permute-start.6 = (f32[4,4,64,1]{3,2,1,0:T(8,128)S(1)}, f32[4,4,64,1]{3,2,1,0:T(8,128)S(1)}, u32[]{:S(2)}, u32[]{:S(2)}) collective-permute-start(f32[4,4,64,1]{3,2,1,0:T(8,128)S(1)} %get-tuple-element.21), channel_id=1, source_target_pairs={{0,1},{1,2},{2,3},{4,5},{5,6},{6,7},{8,9},{9,10},{10,11},{12,13},{... | collective-permute-start | bytes 12296 | tf_op jit(solution)/shard_map/ppermute | solution.py:18
  88.7 1.3 collective-permute-start.7
  90.1 5.5 %collective-permute-done.6 = f32[4,4,64,1]{3,2,1,0:T(8,128)S(1)} collective-permute-done((f32[4,4,64,1]{3,2,1,0:T(8,128)S(1)}, f32[4,4,64,1]{3,2,1,0:T(8,128)S(1)}, u32[]{:S(2)}, u32[]{:S(2)}) %collective-permute-start.6) | collective-permute-done | bytes 4128 | tf_op jit(solution)/shard_map/ppermute | solution.py:18
  95.6 4.2 %collective-permute-done.7 = f32[4,4,64,1]{3,2,1,0:T(8,128)S(1)} collective-permute-done((f32[4,4,64,1]{3,2,1,0:T(8,128)S(1)}, f32[4,4,64,1]{3,2,1,0:T(8,128)S(1)}, u32[]{:S(2)}, u32[]{:S(2)}) %collective-permute-start.7) | collective-permute-done | bytes 4128 | tf_op jit(solution)/shard_map/ppermute | solution.py:21
  99.8 1.5 %select_maximum_fusion = f32[4,4,66,130]{3,2,1,0:T(8,128)S(1)} fusion(f32[4,4,64,1]{3,2,1,0:T(8,128)S(1)} %collective-permute-done.7, f32[4,4,64,1]{3,2,1,0:T(8,128)S(1)} %collective-permute-done.6, f32[4,1,64,128]{3,2,1,0:T(8,128)} %collective-permute-done.5, f32[4,2,64,128]{3,2,1,0:T(8,128)S(1)} %copy-done.3, f32[4,1,64,128]{3,2,1,0:T(8,128)} %collective-permute-done.4), kind=kLoop, calls=%fused_computation.8 | loop fusion | flops 1647360 | bytes 1081600 | tf_op jit(solution)/shard_map/concatenate | solution.py:22
  103.7 1.2 copy-done.1
  106.9 3.4 %all-to-all-start = ((f32[4,2,64,128]{3,1,0,2:T(2,128)}), f32[4,2,64,128]{3,1,0,2:T(2,128)S(1)}, u32[]{:S(2)}, u32[]{:S(2)}) async-start(f32[4,2,64,128]{3,1,0,2:T(2,128)} %copy.8), calls=%async_computation | async-start | bytes 524288 | tf_op jit(solution)/shard_map/all_to_all | solution.py:95
  110.3 31.4 %all-reduce.2 = (f32[4]{0:T(128)S(1)}, f32[4]{0:T(128)S(1)}) all-reduce(f32[4]{0:T(128)S(1)} %get-tuple-element.5, f32[4]{0:T(128)S(1)} %get-tuple-element.4), channel_id=1, replica_groups=mesh['gx'=2,'gy'=4,'gz'=4] {'gy','gz'}, use_global_device_ids=true, to_apply=%region_10.11 | all-reduce | flops 8 | bytes 64 | tf_op jit(solution)/shard_map/psum | solution.py:93
  141.7 4.9 %all-reduce.4 = (f32[4]{0:T(128)S(1)}, f32[4]{0:T(128)S(1)}) all-reduce(f32[4]{0:T(128)S(1)} %get-tuple-element.6, f32[4]{0:T(128)S(1)} %get-tuple-element.7), channel_id=1, replica_groups=mesh['gx'=2,'gy'=4,'gz'=4] {'gx'}, use_global_device_ids=true, to_apply=%region_11.12 | all-reduce | flops 8 | bytes 64 | tf_op jit(solution)/shard_map/psum | solution.py:93
  (73 shorter events, 13.3 us)
Async XLA Ops:
  4.0 4.0 %collective-permute-start = (f32[4,1,64,128]{3,2,1,0:T(8,128)S(1)}, f32[4,1,64,128]{3,2,1,0:T(8,128)S(1)}, u32[]{:S(2)}, u32[]{:S(2)}) collective-permute-start(f32[4,1,64,128]{3,2,1,0:T(8,128)S(1)} %get-tuple-element.28), channel_id=1, source_target_pairs={{0,4},{4,8},{8,12},{12,16},{16,20},{20,24},{24,28},{1,5},{5,9},{9,... | collective-permute-start | bytes 393224 | tf_op jit(solution)/shard_map/ppermute | solution.py:18
  6.4 5.3 %collective-permute-start.1 = (f32[4,1,64,128]{3,2,1,0:T(8,128)S(1)}, f32[4,1,64,128]{3,2,1,0:T(8,128)S(1)}, u32[]{:S(2)}, u32[]{:S(2)}) collective-permute-start(f32[4,1,64,128]{3,2,1,0:T(8,128)S(1)} %get-tuple-element.29), channel_id=1, source_target_pairs={{4,0},{8,4},{12,8},{16,12},{20,16},{24,20},{28,24},{5,1},{9,5},{13... | collective-permute-start | bytes 393224 | tf_op jit(solution)/shard_map/ppermute | solution.py:21
  7.9 23.2 %copy-start.6 = (f32[3,65,129]{2,1,0:T(8,128)}, f32[3,65,129]{2,1,0:T(8,128)S(1)}, u32[]{:S(2)}) copy-start(f32[3,65,129]{2,1,0:T(8,128)S(1)} %and_convert_fusion) | copy-start | bytes 301864
  12.0 13.2 %collective-permute-start.2 = (f32[4,4,64,1]{3,2,1,0:T(8,128)S(1)}, f32[4,4,64,1]{3,2,1,0:T(8,128)S(1)}, u32[]{:S(2)}, u32[]{:S(2)}) collective-permute-start(f32[4,4,64,1]{3,2,1,0:T(8,128)S(1)} %get-tuple-element.23), channel_id=1, source_target_pairs={{0,1},{1,2},{2,3},{4,5},{5,6},{6,7},{8,9},{9,10},{10,11},{12,13},{... | collective-permute-start | bytes 12296 | tf_op jit(solution)/shard_map/ppermute | solution.py:18
  15.5 14.4 %collective-permute-start.3 = (f32[4,4,64,1]{3,2,1,0:T(8,128)S(1)}, f32[4,4,64,1]{3,2,1,0:T(8,128)S(1)}, u32[]{:S(2)}, u32[]{:S(2)}) collective-permute-start(f32[4,4,64,1]{3,2,1,0:T(8,128)S(1)} %get-tuple-element.24), channel_id=1, source_target_pairs={{1,0},{2,1},{3,2},{5,4},{6,5},{7,6},{9,8},{10,9},{11,10},{13,12},{... | collective-permute-start | bytes 12296 | tf_op jit(solution)/shard_map/ppermute | solution.py:21
  16.8 14.1 %copy-start.14 = (pred[65]{0:T(512)(128)(4,1)}, pred[65]{0:T(512)(128)(4,1)S(1)}, u32[]{:S(2)}) copy-start(pred[65]{0:T(512)(128)(4,1)S(1)} %fusion.62) | copy-start | bytes 199
  31.7 0.9 copy-start.9
  32.6 1.5 %copy-start = (f32[4,3,3,65,129]{4,3,2,0,1:T(8,128)}, f32[4,3,3,65,129]{4,3,2,0,1:T(8,128)S(1)}, u32[]{:S(2)}) copy-start(f32[4,3,3,65,129]{4,3,2,0,1:T(8,128)S(1)} %fusion.1) | copy-start | bytes 3622324
  34.1 2.6 %copy-start.11 = (f32[2,64,128]{2,1,0:T(8,128)}, f32[2,64,128]{2,1,0:T(8,128)S(1)}, u32[]{:S(2)}) copy-start(f32[2,64,128]{2,1,0:T(8,128)S(1)} %maximum_bitcast_fusion.1) | copy-start | bytes 196612
  34.1 55.9 %copy-start.13 = (s32[4]{0:T(128)S(1)}, s32[4]{0:T(128)}, u32[]{:S(2)}) copy-start(s32[4]{0:T(128)} %param.3) | copy-start | bytes 52
  36.7 48.0 %collective-permute-start.4 = (f32[4,1,64,128]{3,2,1,0:T(8,128)}, f32[4,1,64,128]{3,2,1,0:T(8,128)}, u32[]{:S(2)}, u32[]{:S(2)}) collective-permute-start(f32[4,1,64,128]{3,2,1,0:T(8,128)} %get-tuple-element.26), channel_id=1, source_target_pairs={{0,4},{4,8},{8,12},{12,16},{16,20},{20,24},{24,28},{1,5},{5,9},{9,... | collective-permute-start | bytes 393224 | tf_op jit(solution)/shard_map/ppermute | solution.py:18
  41.3 43.4 %collective-permute-start.5 = (f32[4,1,64,128]{3,2,1,0:T(8,128)}, f32[4,1,64,128]{3,2,1,0:T(8,128)}, u32[]{:S(2)}, u32[]{:S(2)}) collective-permute-start(f32[4,1,64,128]{3,2,1,0:T(8,128)} %get-tuple-element.27), channel_id=1, source_target_pairs={{4,0},{8,4},{12,8},{16,12},{20,16},{24,20},{28,24},{5,1},{9,5},{13... | collective-permute-start | bytes 393224 | tf_op jit(solution)/shard_map/ppermute | solution.py:21
  84.7 5.3 %copy-start.16 = (f32[4]{0:T(128)S(1)}, f32[4]{0:T(128)}, u32[]{:S(2)}) copy-start(f32[4]{0:T(128)} %get-tuple-element.12) | copy-start | bytes 52
  84.7 5.4 %copy-start.17 = (f32[4]{0:T(128)S(1)}, f32[4]{0:T(128)}, u32[]{:S(2)}) copy-start(f32[4]{0:T(128)} %get-tuple-element.13) | copy-start | bytes 52
  84.7 15.1 %copy-start.3 = (f32[4,2,64,128]{3,2,1,0:T(8,128)S(1)}, f32[4,2,64,128]{3,2,1,0:T(8,128)}, u32[]{:S(2)}) copy-start(f32[4,2,64,128]{3,2,1,0:T(8,128)} %copy-done.2) | copy-start | bytes 786436
  85.8 15.5 %copy-start.15 = (pred[65]{0:T(512)(128)(4,1)S(1)}, pred[65]{0:T(512)(128)(4,1)}, u32[]{:S(2)}) copy-start(pred[65]{0:T(512)(128)(4,1)} %copy-done.14) | copy-start | bytes 199
  86.1 9.5 %collective-permute-start.6 = (f32[4,4,64,1]{3,2,1,0:T(8,128)S(1)}, f32[4,4,64,1]{3,2,1,0:T(8,128)S(1)}, u32[]{:S(2)}, u32[]{:S(2)}) collective-permute-start(f32[4,4,64,1]{3,2,1,0:T(8,128)S(1)} %get-tuple-element.21), channel_id=1, source_target_pairs={{0,1},{1,2},{2,3},{4,5},{5,6},{6,7},{8,9},{9,10},{10,11},{12,13},{... | collective-permute-start | bytes 12296 | tf_op jit(solution)/shard_map/ppermute | solution.py:18
  88.7 11.1 %collective-permute-start.7 = (f32[4,4,64,1]{3,2,1,0:T(8,128)S(1)}, f32[4,4,64,1]{3,2,1,0:T(8,128)S(1)}, u32[]{:S(2)}, u32[]{:S(2)}) collective-permute-start(f32[4,4,64,1]{3,2,1,0:T(8,128)S(1)} %get-tuple-element.22), channel_id=1, source_target_pairs={{1,0},{2,1},{3,2},{5,4},{6,5},{7,6},{9,8},{10,9},{11,10},{13,12},{... | collective-permute-start | bytes 12296 | tf_op jit(solution)/shard_map/ppermute | solution.py:21
  101.8 0.9 copy-start.7
  103.2 1.8 %copy-start.1 = (f32[4,3,3,65,129]{4,3,2,0,1:T(8,128)S(1)}, f32[4,3,3,65,129]{4,3,2,0,1:T(8,128)}, u32[]{:S(2)}) copy-start(f32[4,3,3,65,129]{4,3,2,0,1:T(8,128)} %copy-done) | copy-start | bytes 3622324
  103.2 1.7 %copy-start.5 = (f32[2,64,128]{2,1,0:T(8,128)S(1)}, f32[2,64,128]{2,1,0:T(8,128)}, u32[]{:S(2)}) copy-start(f32[2,64,128]{2,1,0:T(8,128)} %param.2) | copy-start | bytes 196612
  103.2 1.7 %copy-start.10 = (f32[2,64,128]{2,1,0:T(8,128)S(1)}, f32[2,64,128]{2,1,0:T(8,128)}, u32[]{:S(2)}) copy-start(f32[2,64,128]{2,1,0:T(8,128)} %copy-done.8) | copy-start | bytes 196612
  103.2 1.7 %copy-start.12 = (f32[2,64,128]{2,1,0:T(8,128)S(1)}, f32[2,64,128]{2,1,0:T(8,128)}, u32[]{:S(2)}) copy-start(f32[2,64,128]{2,1,0:T(8,128)} %copy-done.11) | copy-start | bytes 196612
  106.9 40.2 %all-to-all-start = ((f32[4,2,64,128]{3,1,0,2:T(2,128)}), f32[4,2,64,128]{3,1,0,2:T(2,128)S(1)}, u32[]{:S(2)}, u32[]{:S(2)}) async-start(f32[4,2,64,128]{3,1,0,2:T(2,128)} %copy.8), calls=%async_computation | async-start | bytes 524288 | tf_op jit(solution)/shard_map/all_to_all | solution.py:95
  (3 other events, 2.2 us)
